TPU v7x, 256 devices: a whole 4x4x8 slice. The times are simulated.
256 devices in a mesh: shard: 32 (over y, x, core), dp: 8 (over z).
Axes of the slice: x: 4, y: 4, z: 8, core: 2. Of those that a mesh axis runs over, the one named last changes fastest.
Arguments:
- grad: float32 [288, 128, 4096], P('shard', 'dp'), may hold values from -252 to 252
- param: bfloat16 [288, 128, 4096], P('shard', 'dp'), may hold values from -0.119628906 to 0.119628906
- row_state: float32 [288, 128], P('shard', 'dp'), may hold values from 0.3 to 27
- col_state: float32 [3, 4096], replicated, may hold values from 0.002 to 400
- block_start: int32 [32], replicated, may hold values from 0 to 143, as said below
- block_matrix: int32 [144], replicated, may hold values from 0 to 2, as said below
- step: int32 [1], replicated, may hold values from 2 to 11
Outputs:
- new_params: bfloat16 [18432, 4096], P(None, 'shard')
- new_row_state: float32 [288, 128], P('shard', 'dp')
- new_col_state: float32 [3, 4096], replicated
Inputs may be any that keep to these rules, and one draw needn't show every extreme that they name: block_start rises from 0 at index 0; every shard index owns between 1 and 9 consecutive global blocks, held in its first slots, and some index owns exactly 9; slots past a device's owned count hold values that no output reads. `block_matrix`: ids 0 and 1 each label 4096 / 128 blocks and id 2 labels 10240 / 128 blocks, in any order.
All inputs are finite; a program needn't handle non-finite values.
Results may differ from a plain program's by a relative error of at most 0.0004.
Values may be sent and summed in bfloat16 or wider, within the bound.
A program may use at most 64 MiB of HBM per device.

v0:
```python
import jax
import jax.numpy as jnp
from jax import lax
from jax.sharding import Mesh
from jax.sharding import PartitionSpec as P

D = 4096
FF = 10240
SHARD = ("shard_0", "shard_1", "shard_2")


def cut_along(shard, dim, length):
    shape = shard.shape
    blocks = shard.reshape(*shape[:dim], length, shape[dim] // length, *shape[dim + 1 :])
    return jnp.moveaxis(blocks, dim, 0)


def summed_on_arrival(shard, axis, dim):
    length = lax.axis_size(axis)
    blocks = lax.all_to_all(cut_along(shard, dim, length), axis, 0, 0, tiled=True)
    return jnp.sum(blocks, axis=0)


def summed_rows(shard, axes, dim):
    far, near = axes
    blocks = cut_along(shard, dim, lax.axis_size(far))
    nearer = summed_on_arrival(blocks, near, dim + 1)
    arrived = lax.all_to_all(nearer, far, split_axis=0, concat_axis=0, tiled=True)
    return arrived.sum(axis=0)


def filled_up(lines, length):
    spare = -lines.shape[0] % length
    if not spare:
        return lines
    return jnp.concatenate([lines, jnp.zeros((spare, *lines.shape[1:]), lines.dtype)])


def sent_to_all(shard, axis):
    copies = jnp.broadcast_to(shard, (lax.axis_size(axis), *shard.shape))
    return lax.all_to_all(copies, axis, split_axis=0, concat_axis=0, tiled=True)


def in_order(blocks, dim):
    shape = list(blocks.shape[1:])
    shape[dim] *= blocks.shape[0]
    return jnp.moveaxis(blocks, 0, dim).reshape(shape)


def whole_of(shard, axes, dim):
    far, near = axes
    blocks = sent_to_all(sent_to_all(shard, far), near)
    return in_order(blocks.swapaxes(0, 1).reshape(-1, *shard.shape), dim)


def sum_by_parts(shard, axes):
    own = summed_rows(filled_up(shard, lax.axis_size(axes[0]) * lax.axis_size(axes[1])), axes, 0)
    whole = whole_of(own, axes, 0)
    return whole[: len(shard)].reshape(shard.shape)


def together(arrays, axis):
    ravelled, at, gathered = (jnp.concatenate([a.reshape(-1) for a in arrays]), 0, [])
    subtotal = sum_by_parts(ravelled, axis)
    for a in arrays:
        gathered.append(subtotal[at : at + a.size].reshape(a.shape))
        at += a.size
    return tuple(gathered)


def moved_by_axis(blocks, axes, turns):
    shape = [lax.axis_size(a) for a in axes]
    blocks = blocks.reshape(*shape, *blocks.shape[1:])
    for k in turns:
        blocks = lax.all_to_all(blocks, axes[k], split_axis=k, concat_axis=k, tiled=True)
    return blocks.reshape(-1, *blocks.shape[len(axes) :])


def exchange_by_chip(shard, groups, turns, split_dim, concat_dim):
    length = lax.axis_size(groups[0]) * lax.axis_size(groups[1])
    blocks = cut_along(shard, split_dim, length)
    return in_order(moved_by_axis(blocks, groups, turns), concat_dim)


def scale_grad(grad, safe_rows, matrix_pick, new_cols, row_avg):
    slot_cols = jnp.dot(matrix_pick, new_cols, precision=lax.Precision.HIGHEST)
    slot_avg = jnp.dot(matrix_pick, row_avg, precision=lax.Precision.HIGHEST)
    return grad / jnp.sqrt(safe_rows[:, :, None] * slot_cols[:, None, :] / slot_avg[:, None, None])


def body(grad, param, row_state, col_state, block_start, block_matrix, step):
    slot_count = grad.shape[0]
    total_blocks = block_matrix.shape[0]
    shard_index = lax.axis_index(SHARD)
    block_ends = jnp.concatenate([block_start[1:], jnp.full((1,), total_blocks, jnp.int32)])
    first_block = lax.dynamic_index_in_dim(block_start, shard_index, keepdims=False)
    owned_count = lax.dynamic_index_in_dim(block_ends, shard_index, keepdims=False) - first_block
    slot_ids = jnp.arange(slot_count, dtype=jnp.int32)
    live_slot = slot_ids < owned_count
    block_ids = first_block + slot_ids
    block_table = block_ids[:, None] == jnp.arange(total_blocks, dtype=jnp.int32)[None, :]
    matrix_ids = jnp.sum(jnp.where(block_table, block_matrix[None, :], 0), axis=1)
    matrix_ids = jnp.where(live_slot, matrix_ids, 0)
    matrix_pick = (matrix_ids[:, None] == jnp.arange(3, dtype=jnp.int32)[None, :]).astype(
        jnp.float32
    )
    member = matrix_pick * live_slot[:, None].astype(jnp.float32)
    row_count = jnp.array([D, D, FF], jnp.float32)
    step_value = step[0].astype(jnp.float32)
    decay_rate = 1.0 - step_value ** (-0.8)
    learn_rate = 1.0 / jnp.sqrt(jnp.maximum(step_value, 10000.0))
    squares = grad * grad
    new_rows = jnp.where(
        live_slot[:, None],
        decay_rate * row_state + (1.0 - decay_rate) * jnp.sum(squares, axis=2) / D,
        0.0,
    )
    safe_rows = jnp.where(live_slot[:, None], new_rows, 1.0)
    col_part = jnp.einsum(
        "sm,sd->md", member, jnp.sum(squares, axis=1), precision=lax.Precision.HIGHEST
    )
    row_part = jnp.dot(jnp.sum(new_rows, axis=1), member, precision=lax.Precision.HIGHEST)
    quot_part = jnp.einsum(
        "sm,sd->md",
        member,
        jnp.sum(squares / safe_rows[:, :, None], axis=1),
        precision=lax.Precision.HIGHEST,
    )
    col_total, quot_total, row_total = together(
        (col_part, quot_part, row_part), (("shard_0", "shard_1"), ("shard_2", "dp"))
    )
    new_cols = decay_rate * col_state + (1.0 - decay_rate) * col_total / row_count[:, None]
    row_avg = row_total / row_count
    scaled = scale_grad(grad, safe_rows, matrix_pick, new_cols, row_avg)
    square_total = row_avg * jnp.sum(quot_total / new_cols, axis=1)
    clip_factor = jnp.maximum(1.0, jnp.sqrt(square_total / (row_count * D)))
    slot_clip = jnp.dot(matrix_pick, clip_factor, precision=lax.Precision.HIGHEST)
    updated = jnp.where(
        live_slot[:, None, None],
        param.astype(jnp.float32) - learn_rate * scaled / slot_clip[:, None, None],
        0.0,
    ).astype(jnp.bfloat16)
    column_rows = exchange_by_chip(updated, (("shard_0", "shard_1"), "shard_2"), (1, 0), 2, 0)
    spread = lax.all_gather(column_rows, "dp", axis=1, tiled=True)
    block_index = jnp.arange(total_blocks, dtype=jnp.int32)
    block_owner = (
        jnp.sum((block_start[None, :] <= block_index[:, None]).astype(jnp.int32), axis=1) - 1
    )
    slot_of = block_owner * slot_count + block_index - jnp.take(block_start, block_owner)
    new_params = jnp.take(spread, slot_of, axis=0).reshape(
        total_blocks * spread.shape[1], spread.shape[2]
    )
    return (new_params, new_rows, new_cols)


def solution(mesh):
    finer = Mesh(
        mesh.devices.reshape(4, 4, 2, mesh.shape["dp"]), ("shard_0", "shard_1", "shard_2", "dp")
    )
    in_specs = (P(SHARD, "dp", None), P(SHARD, "dp", None), P(SHARD, "dp"), P(), P(), P(), P())
    out_specs = (P(None, SHARD), P(SHARD, "dp"), P())
    return jax.shard_map(body, mesh=finer, in_specs=in_specs, out_specs=out_specs, check_vma=False)
```

profile of v0, /device:TPU:2, one launch (start us, length us, event | category | flops | bytes accessed | tf_op | source)
XLA Modules:
  0.0 263.2 jit_solution(12649364172545486583)
XLA Ops:
  7.2 0.9 slice.16
  8.1 1.2 dynamic_slice.8
  9.3 0.1 pad_add_fusion
  9.4 0.6 dynamic_slice.7
  10.0 1.2 iota_add_fusion
  13.1 1.9 multiply_reduce_fusion.1
  15.1 0.8 fusion.32
  15.9 0.1 broadcast_select_fusion
  15.9 0.5 copy-done.4
  16.5 1.6 divide_reduce_fusion
  18.1 0.9 select_reduce_fusion
  19.0 1.0 fusion.1
  20.1 1.5 reshape.144
  21.5 2.0 fusion.3
  23.5 1.5 reshape.143
  25.0 1.4 convolution_bitcast_fusion.2
  26.4 1.5 concatenate.7
  27.9 1.8 reshape_reshape.9
  29.7 0.9 copy.23
  30.7 17.0 %all_to_all.38 = f32[16,16,97]{2,1,0:T(8,128)} all-to-all(f32[16,16,97]{2,1,0:T(8,128)S(1)} %copy.23), channel_id=1, replica_groups=mesh['shard_0'=4,'shard_1'=4,'shard_2'=2,'dp'=8] {'shard_2','dp'}, dimensions={0} | all-to-all | bytes 198656 | tf_op jit(solution)/shard_map/all_to_all | solution.py:20
  47.7 0.9 reduce_sum.87
  48.6 13.6 %all_to_all.39 = f32[16,1,97]{2,1,0:T(1,128)} all-to-all(f32[16,1,97]{2,1,0:T(1,128)S(1)} %bitcast.48), channel_id=1, replica_groups=mesh['shard_0'=4,'shard_1'=4,'shard_2'=2,'dp'=8] {'shard_0','shard_1'}, dimensions={0} | all-to-all | bytes 12416 | tf_op jit(solution)/shard_map/all_to_all | solution.py:28
  62.2 0.7 reduce_sum.88
  63.0 10.6 %all_to_all.40 = f32[16,1,97]{2,1,0:T(1,128)S(1)} all-to-all(f32[16,1,97]{2,1,0:T(1,128)S(1)} %broadcast_in_dim.106), channel_id=1, replica_groups=mesh['shard_0'=4,'shard_1'=4,'shard_2'=2,'dp'=8] {'shard_0','shard_1'}, dimensions={0} | all-to-all | bytes 12416 | tf_op jit(solution)/shard_map/all_to_all | solution.py:41
  73.5 0.7 broadcast_in_dim.107
  74.2 4.2 %all-to-all-start.3 = ((f32[16,16,97]{2,1,0:T(8,128)}), f32[16,16,97]{2,1,0:T(8,128)}, u32[]{:S(2)}, u32[]{:S(2)}) async-start(f32[16,16,97]{2,1,0:T(8,128)} %broadcast_in_dim.107), calls=%async_computation.3 | async-start | bytes 262144 | tf_op jit(solution)/shard_map/all_to_all | solution.py:41
  78.5 8.4 %all-to-all-done.3 = f32[16,16,97]{2,1,0:T(8,128)} async-done(((f32[16,16,97]{2,1,0:T(8,128)}), f32[16,16,97]{2,1,0:T(8,128)}, u32[]{:S(2)}, u32[]{:S(2)}) %all-to-all-start.3) | async-done | bytes 99360 | tf_op jit(solution)/shard_map/all_to_all | solution.py:41
  86.8 1.6 copy.24
  88.4 1.7 reshape_reshape.10
  90.2 1.5 slice_multiply_fusion
  91.6 1.4 mul.105
  93.1 1.4 reshape.145
  94.5 0.9 convolution_bitcast_fusion.1
  95.4 1.2 divide_reduce_fusion.1
  96.6 1.0 fusion.5
  97.6 0.9 convolution_bitcast_fusion
  98.5 1.6 select_convert_fusion
  100.1 0.2 copy.30
  100.4 0.5 copy.26
  100.8 4.7 %all_to_all.41 = bf16[16,2,9,16,128]{4,3,2,0,1:T(8,128)(2,1)S(1)} all-to-all(bf16[16,2,9,16,128]{4,3,2,0,1:T(8,128)(2,1)S(1)} %copy.26), channel_id=1, replica_groups=mesh['shard_0'=4,'shard_1'=4,'shard_2'=2,'dp'=8] {'shard_2'}, dimensions={1} | all-to-all | bytes 2359296 | tf_op jit(solution)/shard_map/all_to_all | solution.py:75
  105.5 0.2 copy.27
  105.7 22.5 %all_to_all.42 = bf16[16,2,9,16,128]{4,3,2,1,0:T(8,128)(2,1)} all-to-all(bf16[16,2,9,16,128]{4,3,2,1,0:T(8,128)(2,1)S(1)} %copy.27), channel_id=1, replica_groups=mesh['shard_0'=4,'shard_1'=4,'shard_2'=2,'dp'=8] {'shard_0','shard_1'}, dimensions={0} | all-to-all | bytes 2359296 | tf_op jit(solution)/shard_map/all_to_all | solution.py:75
  128.3 0.1 convert_reduce_fusion
  128.4 1.6 gather_fusion
  130.0 0.1 broadcast_bitcast_fusion
  130.1 101.9 %all-gather.2.cloned.1.call-done = bf16[288,128,128]{2,1,0:T(8,128)(2,1)} async-done(((bf16[288,16,128]{2,1,0:T(8,128)(2,1)}), bf16[288,128,128]{2,1,0:T(8,128)(2,1)}) %all-gather.2.cloned.1.call-update) | async-done | bytes 9437200 | tf_op jit(solution)/shard_map/all_gather | solution.py:144
  232.0 11.3 %gather_fusion.1 = bf16[144,128,128]{2,1,0:T(8,128)(2,1)} fusion(bf16[288,128,128]{2,1,0:T(8,128)(2,1)} %all-gather.2.cloned.1.call-done, s32[1024]{0:T(1024)S(1)} %pad_clamp_fusion), kind=kCustom, calls=%fused_computation.1 | custom fusion | bytes 9437760 | tf_op jit(solution)/shard_map/jit(_take)/gather | solution.py:150
  243.3 13.0 %bitcast_select_fusion = bf16[18432,128]{1,0:T(8,128)(2,1)} fusion(bf16[144,128,128]{2,1,0:T(8,128)(2,1)} %gather_fusion.1, pred[18432]{0:T(1024)(128)(4,1)S(1)} %broadcast_bitcast_fusion), kind=kLoop, calls=%fused_computation.2 | loop fusion | flops 2359296 | bytes 9455616 | tf_op jit(solution)/shard_map/jit(_take)/select_n | solution.py:150
  (29 shorter events, 0.2 us)
Async XLA Ops:
  7.2 9.3 %copy-start.1 = (f32[9,16,4096]{2,1,0:T(8,128)S(1)}, f32[9,16,4096]{2,1,0:T(8,128)}, u32[]{:S(2)}) copy-start(f32[9,16,4096]{2,1,0:T(8,128)} %param.8) | copy-start | bytes 7077892
  7.2 7.9 %copy-start.5 = (f32[9,16]{1,0:T(8,128)S(1)}, f32[9,16]{1,0:T(8,128)}, u32[]{:S(2)}) copy-start(f32[9,16]{1,0:T(8,128)} %param.10) | copy-start | bytes 1732
  12.4 3.5 %copy-start.7 = (pred[9]{0:T(512)(128)(4,1)}, pred[9]{0:T(512)(128)(4,1)S(1)}, u32[]{:S(2)}) copy-start(pred[9]{0:T(512)(128)(4,1)S(1)} %get-tuple-element.13) | copy-start | bytes 31
  13.1 5.0 %copy-start.8 = (s32[144]{0:T(256)S(1)}, s32[144]{0:T(256)}, u32[]{:S(2)}) copy-start(s32[144]{0:T(256)} %param.13) | copy-start | bytes 1732
  15.9 0.6 copy-start.4
  18.1 80.4 %copy-start.2 = (bf16[9,16,4096]{2,1,0:T(8,128)(2,1)S(1)}, bf16[9,16,4096]{2,1,0:T(8,128)(2,1)}, u32[]{:S(2)}) copy-start(bf16[9,16,4096]{2,1,0:T(8,128)(2,1)} %param.9) | copy-start | bytes 3538948
  19.0 11.6 %copy-start.6 = (s32[9]{0:T(128)}, s32[9]{0:T(128)S(1)}, u32[]{:S(2)}) copy-start(s32[9]{0:T(128)S(1)} %broadcast_select_fusion.1) | copy-start | bytes 112
  74.2 12.7 %all-to-all-start.3 = ((f32[16,16,97]{2,1,0:T(8,128)}), f32[16,16,97]{2,1,0:T(8,128)}, u32[]{:S(2)}, u32[]{:S(2)}) async-start(f32[16,16,97]{2,1,0:T(8,128)} %broadcast_in_dim.107), calls=%async_computation.3 | async-start | bytes 262144 | tf_op jit(solution)/shard_map/all_to_all | solution.py:41
  78.4 153.6 %all-gather.2.cloned.1.call-start = ((), (), s32[]{:S(2)}) async-start(), calls=%async_computation.6 | async-start | bytes 10616832 | tf_op jit(solution)/shard_map/all_gather | solution.py:144
  96.6 1.9 copy-start.3
  105.7 22.5 %copy-start = (s32[32]{0:T(128)S(1)}, s32[32]{0:T(128)}, u32[]{:S(2)}) copy-start(s32[32]{0:T(128)} %param.12) | copy-start | bytes 388
Sparse Core Ops, SparseCore 0:
  128.4 103.5 all-gather.1
where the time goes:
time: 265 us; the launch traced here: 263 us
  waiting for transfers between devices  110 us (42%)
  blocking collectives  68.3 us (26%)
  local copies, waits for them, and re-layouts  31.3 us (12%)
  other arithmetic  25.5 us (10%)
  between operations  16.3 us (6%)
  matrix products  7.16 us (3%)
  starting transfers between devices  4.21 us (2%)
    all_gather x1, waiting for transfers between devices, body(): spread = lax.all_gather(column_rows, 'dp', axis=1, tiled=True)  102 us
    all_to_all x2, blocking collectives, moved_by_axis(): lax.all_to_all(blocks, axes[k], split_axis=k, concat_axis=k, tiled=True)  27.2 us
    all_to_all x1, blocking collectives, summed_on_arrival(): lax.all_to_all(cut_along(shard, dim, length), axis, 0, 0, tiled=True)  17 us
    all_to_all x1, blocking collectives, summed_rows(): lax.all_to_all(nearer, far, split_axis=0, concat_axis=0, tiled=True)  13.6 us
    select_n x2, other arithmetic, body(): jnp.take(spread, slot_of, axis=0)  13 us
    gather x1, local copies, waits for them, and re-layouts, body(): jnp.take(spread, slot_of, axis=0)  11.3 us
    all_to_all x1, blocking collectives, sent_to_all(): return lax.all_to_all(copies, axis, split_axis=0, concat_axis=0, tiled=True)  10.6 us
    all_to_all x1, waiting for transfers between devices, sent_to_all(): return lax.all_to_all(copies, axis, split_axis=0, concat_axis=0, tiled=True)  8.38 us
  transfers between devices with their start and end apart: 2, of which 2 were waited for; matrix products, arithmetic and copies ran while one was open for 1% of the time, Pallas kernels for 0%

commit v1 on v0

--- a/solution.py
+++ b/solution.py
@@ -141,7 +141,9 @@
         0.0,
     ).astype(jnp.bfloat16)
     column_rows = exchange_by_chip(updated, (("shard_0", "shard_1"), "shard_2"), (1, 0), 2, 0)
-    spread = lax.all_gather(column_rows, "dp", axis=1, tiled=True)
+    spread = jnp.concatenate(
+        lax.all_to_all(jnp.stack([column_rows] * lax.axis_size("dp")), "dp", 0, 0), axis=1
+    )
     block_index = jnp.arange(total_blocks, dtype=jnp.int32)
     block_owner = (
         jnp.sum((block_start[None, :] <= block_index[:, None]).astype(jnp.int32), axis=1) - 1

time: 265 us -> 377 us (1.42)
  waiting for transfers between devices: 110 us -> 215 us
  local copies, waits for them, and re-layouts: 31.3 us -> 46.2 us
  between operations: 16.3 us -> 2.94 us
  starting transfers between devices: 4.21 us -> 9.51 us
    all_to_all x0 -> x1, waiting for transfers between devices: none -> 206 us  [body(): lax.all_to_all(jnp.stack([column_rows] * lax.axis_size('dp')), 'dp', 0, 0)]
    all_gather x1 -> x0, waiting for transfers between devices: 102 us -> none  [body(): spread = lax.all_gather(column_rows, 'dp', axis=1, tiled=True)]
    all_to_all x0 -> x1, local copies, waits for them, and re-layouts: none -> 10.1 us  [body(): lax.all_to_all(jnp.stack([column_rows] * lax.axis_size('dp')), 'dp', 0, 0)]
    all_to_all x0 -> x1, starting transfers between devices: none -> 5.34 us  [body(): lax.all_to_all(jnp.stack([column_rows] * lax.axis_size('dp')), 'dp', 0, 0)]
    another operation x0 -> x1, local copies, waits for them, and re-layouts: none -> 4.87 us  [body(): jnp.stack([column_rows] * lax.axis_size('dp'))]
  transfers between devices with their start and end apart: 2 -> 2, of which waited for: 2 -> 2; matrix products, arithmetic and copies ran while one was open for 1% -> 0% of each run, Pallas kernels for 0% -> 0%
where the time goes in v1:
time: 377 us; the launch traced here: 374 us
  waiting for transfers between devices  215 us (57%)
  blocking collectives  67.7 us (18%)
  local copies, waits for them, and re-layouts  46.2 us (12%)
  other arithmetic  25.5 us (7%)
  starting transfers between devices  9.51 us (3%)
  matrix products  7.16 us (2%)
    all_to_all x1, waiting for transfers between devices, body(): lax.all_to_all(jnp.stack([column_rows] * lax.axis_size('dp')), 'dp', 0, 0)  206 us
    all_to_all x2, blocking collectives, moved_by_axis(): lax.all_to_all(blocks, axes[k], split_axis=k, concat_axis=k, tiled=True)  26.5 us
    all_to_all x1, blocking collectives, summed_on_arrival(): lax.all_to_all(cut_along(shard, dim, length), axis, 0, 0, tiled=True)  17 us
    all_to_all x1, blocking collectives, summed_rows(): lax.all_to_all(nearer, far, split_axis=0, concat_axis=0, tiled=True)  13.6 us
    select_n x2, other arithmetic, body(): jnp.take(spread, slot_of, axis=0)  13 us
    gather x1, local copies, waits for them, and re-layouts, body(): jnp.take(spread, slot_of, axis=0)  11.2 us
    all_to_all x1, blocking collectives, sent_to_all(): return lax.all_to_all(copies, axis, split_axis=0, concat_axis=0, tiled=True)  10.6 us
    all_to_all x1, local copies, waits for them, and re-layouts, body(): lax.all_to_all(jnp.stack([column_rows] * lax.axis_size('dp')), 'dp', 0, 0)  10.1 us
  transfers between devices with their start and end apart: 2, of which 2 were waited for; matrix products, arithmetic and copies ran while one was open for 0% of the time, Pallas kernels for 0%

profile of v1, /device:TPU:2, one launch (start us, length us, event | category | flops | bytes accessed | tf_op | source)
XLA Modules:
  0.0 373.7 jit_solution(1401741698100877678)
XLA Ops:
  0.7 0.9 slice.16
  1.5 1.2 dynamic_slice.8
  2.9 0.6 dynamic_slice.7
  3.4 1.2 iota_add_fusion
  6.6 1.9 multiply_reduce_fusion.1
  8.6 0.8 fusion.32
  9.4 0.5 copy-done.4
  9.9 1.6 divide_reduce_fusion
  11.5 0.9 select_reduce_fusion
  12.5 1.0 fusion.1
  13.5 1.5 reshape.152
  15.0 2.0 fusion.3
  17.0 1.5 reshape.151
  18.5 1.4 convolution_bitcast_fusion.2
  19.9 1.5 concatenate.7
  21.4 1.8 reshape_reshape.6
  23.2 0.9 copy.26
  24.1 17.0 %all_to_all.43 = f32[16,16,97]{2,1,0:T(8,128)} all-to-all(f32[16,16,97]{2,1,0:T(8,128)S(1)} %copy.26), channel_id=1, replica_groups=mesh['shard_0'=4,'shard_1'=4,'shard_2'=2,'dp'=8] {'shard_2','dp'}, dimensions={0} | all-to-all | bytes 198656 | tf_op jit(solution)/shard_map/all_to_all | solution.py:20
  41.2 0.9 reduce_sum.87
  42.1 13.6 %all_to_all.44 = f32[16,1,97]{2,1,0:T(1,128)} all-to-all(f32[16,1,97]{2,1,0:T(1,128)S(1)} %bitcast.52), channel_id=1, replica_groups=mesh['shard_0'=4,'shard_1'=4,'shard_2'=2,'dp'=8] {'shard_0','shard_1'}, dimensions={0} | all-to-all | bytes 12416 | tf_op jit(solution)/shard_map/all_to_all | solution.py:28
  55.7 0.7 reduce_sum.88
  56.4 10.6 %all_to_all.45 = f32[16,1,97]{2,1,0:T(1,128)S(1)} all-to-all(f32[16,1,97]{2,1,0:T(1,128)S(1)} %broadcast_in_dim.106), channel_id=1, replica_groups=mesh['shard_0'=4,'shard_1'=4,'shard_2'=2,'dp'=8] {'shard_0','shard_1'}, dimensions={0} | all-to-all | bytes 12416 | tf_op jit(solution)/shard_map/all_to_all | solution.py:41
  67.0 0.7 broadcast_in_dim.107
  67.7 4.2 %all-to-all-start.3 = ((f32[16,16,97]{2,1,0:T(8,128)}), f32[16,16,97]{2,1,0:T(8,128)}, u32[]{:S(2)}, u32[]{:S(2)}) async-start(f32[16,16,97]{2,1,0:T(8,128)} %broadcast_in_dim.107), calls=%async_computation.3 | async-start | bytes 262144 | tf_op jit(solution)/shard_map/all_to_all | solution.py:41
  71.9 8.4 %all-to-all-done.3 = f32[16,16,97]{2,1,0:T(8,128)} async-done(((f32[16,16,97]{2,1,0:T(8,128)}), f32[16,16,97]{2,1,0:T(8,128)}, u32[]{:S(2)}, u32[]{:S(2)}) %all-to-all-start.3) | async-done | bytes 99360 | tf_op jit(solution)/shard_map/all_to_all | solution.py:41
  80.3 1.6 copy.27
  81.9 1.7 reshape_reshape.7
  83.7 1.5 slice_multiply_fusion
  85.1 1.4 mul.105
  86.6 1.4 reshape.153
  88.0 0.9 convolution_bitcast_fusion.1
  88.9 1.2 divide_reduce_fusion.1
  90.1 1.0 fusion.5
  91.0 0.9 convolution_bitcast_fusion
  92.0 1.6 select_convert_fusion
  93.6 0.2 copy.34
  93.8 0.5 copy.29
  94.3 4.7 %all_to_all.46 = bf16[16,2,9,16,128]{4,3,2,0,1:T(8,128)(2,1)S(1)} all-to-all(bf16[16,2,9,16,128]{4,3,2,0,1:T(8,128)(2,1)S(1)} %copy.29), channel_id=1, replica_groups=mesh['shard_0'=4,'shard_1'=4,'shard_2'=2,'dp'=8] {'shard_2'}, dimensions={1} | all-to-all | bytes 2359296 | tf_op jit(solution)/shard_map/all_to_all | solution.py:75
  99.0 0.2 copy.30
  99.2 21.8 %all_to_all.47 = bf16[16,2,9,16,128]{4,3,2,1,0:T(8,128)(2,1)S(1)} all-to-all(bf16[16,2,9,16,128]{4,3,2,1,0:T(8,128)(2,1)S(1)} %copy.30), channel_id=1, replica_groups=mesh['shard_0'=4,'shard_1'=4,'shard_2'=2,'dp'=8] {'shard_0','shard_1'}, dimensions={0} | all-to-all | bytes 2359296 | tf_op jit(solution)/shard_map/all_to_all | solution.py:75
  121.0 4.9 %stack.3 = bf16[8,288,16,128]{3,2,1,0:T(8,128)(2,1)} broadcast(bf16[288,16,128]{2,1,0:T(8,128)(2,1)S(1)} %bitcast.50), dimensions={1,2,3} | broadcast | bytes 10616832 | tf_op jit(solution)/shard_map/stack | solution.py:145
  125.9 5.3 %all-to-all-start.6 = ((bf16[8,288,16,128]{3,2,1,0:T(8,128)(2,1)}), bf16[8,288,16,128]{3,2,1,0:T(8,128)(2,1)}, u32[]{:S(2)}, u32[]{:S(2)}) async-start(bf16[8,288,16,128]{3,2,1,0:T(8,128)(2,1)} %stack.3), calls=%async_computation.6 | async-start | bytes 18874368 | tf_op jit(solution)/shard_map/all_to_all | solution.py:145
  131.3 0.1 convert_reduce_fusion
  131.4 1.6 gather_fusion
  133.1 206.2 %all-to-all-done.6 = bf16[8,288,16,128]{3,2,1,0:T(8,128)(2,1)} async-done(((bf16[8,288,16,128]{3,2,1,0:T(8,128)(2,1)}), bf16[8,288,16,128]{3,2,1,0:T(8,128)(2,1)}, u32[]{:S(2)}, u32[]{:S(2)}) %all-to-all-start.6) | async-done | bytes 9437216 | tf_op jit(solution)/shard_map/all_to_all | solution.py:145
  339.3 10.1 %copy.31 = bf16[8,288,16,128]{3,2,0,1:T(8,128)(2,1)} copy(bf16[8,288,16,128]{3,2,1,0:T(8,128)(2,1)} %all-to-all-done.6) | data formatting | bytes 18874368 | tf_op jit(solution)/shard_map/all_to_all | solution.py:145
  349.5 11.2 %gather_fusion.1 = bf16[144,128,128]{2,1,0:T(8,128)(2,1)} fusion(bf16[288,128,128]{2,1,0:T(8,128)(2,1)} %bitcast.47, s32[1024]{0:T(1024)S(1)} %pad_clamp_fusion), kind=kCustom, calls=%fused_computation.1 | custom fusion | bytes 9437760 | tf_op jit(solution)/shard_map/jit(_take)/gather | solution.py:152
  360.7 13.0 %bitcast_select_fusion = bf16[18432,128]{1,0:T(8,128)(2,1)} fusion(bf16[144,128,128]{2,1,0:T(8,128)(2,1)} %gather_fusion.1, pred[18432]{0:T(1024)(128)(4,1)S(1)} %broadcast_bitcast_fusion), kind=kLoop, calls=%fused_computation.2 | loop fusion | flops 2359296 | bytes 9455616 | tf_op jit(solution)/shard_map/jit(_take)/select_n | solution.py:152
  (30 shorter events, 0.3 us)
Async XLA Ops:
  0.6 9.3 %copy-start.1 = (f32[9,16,4096]{2,1,0:T(8,128)S(1)}, f32[9,16,4096]{2,1,0:T(8,128)}, u32[]{:S(2)}) copy-start(f32[9,16,4096]{2,1,0:T(8,128)} %param.8) | copy-start | bytes 7077892
  0.6 7.9 %copy-start.5 = (f32[9,16]{1,0:T(8,128)S(1)}, f32[9,16]{1,0:T(8,128)}, u32[]{:S(2)}) copy-start(f32[9,16]{1,0:T(8,128)} %param.10) | copy-start | bytes 1732
  5.9 3.5 copy-start.7
  6.6 5.0 %copy-start.8 = (s32[144]{0:T(256)S(1)}, s32[144]{0:T(256)}, u32[]{:S(2)}) copy-start(s32[144]{0:T(256)} %param.13) | copy-start | bytes 1732
  9.3 0.6 copy-start.4
  11.5 80.4 %copy-start.2 = (bf16[9,16,4096]{2,1,0:T(8,128)(2,1)S(1)}, bf16[9,16,4096]{2,1,0:T(8,128)(2,1)}, u32[]{:S(2)}) copy-start(bf16[9,16,4096]{2,1,0:T(8,128)(2,1)} %param.9) | copy-start | bytes 3538948
  12.5 11.7 %copy-start.6 = (s32[9]{0:T(128)}, s32[9]{0:T(128)S(1)}, u32[]{:S(2)}) copy-start(s32[9]{0:T(128)S(1)} %broadcast_select_fusion.1) | copy-start | bytes 112
  67.7 12.7 %all-to-all-start.3 = ((f32[16,16,97]{2,1,0:T(8,128)}), f32[16,16,97]{2,1,0:T(8,128)}, u32[]{:S(2)}, u32[]{:S(2)}) async-start(f32[16,16,97]{2,1,0:T(8,128)} %broadcast_in_dim.107), calls=%async_computation.3 | async-start | bytes 262144 | tf_op jit(solution)/shard_map/all_to_all | solution.py:41
  90.1 1.9 copy-start.3
  125.9 5.4 %copy-start = (s32[32]{0:T(128)S(1)}, s32[32]{0:T(128)}, u32[]{:S(2)}) copy-start(s32[32]{0:T(128)} %param.12) | copy-start | bytes 388
  125.9 213.4 %all-to-all-start.6 = ((bf16[8,288,16,128]{3,2,1,0:T(8,128)(2,1)}), bf16[8,288,16,128]{3,2,1,0:T(8,128)(2,1)}, u32[]{:S(2)}, u32[]{:S(2)}) async-start(bf16[8,288,16,128]{3,2,1,0:T(8,128)(2,1)} %stack.3), calls=%async_computation.6 | async-start | bytes 18874368 | tf_op jit(solution)/shard_map/all_to_all | solution.py:145
